TPU v7x, 32 devices: a whole 2x2x4 slice. The times are simulated.
32 devices in a mesh: row: 2 (over core), col: 8 (over z, x), grp: 2 (over y).
Axes of the slice: x: 2, y: 2, z: 4, core: 2. Of those that a mesh axis runs over, the one named last changes fastest.
Arguments:
- momentum: float32 [2, 4096, 16384], P('grp', 'row', 'col'), may hold values from -6 to 6
- gradient: bfloat16 [2, 4096, 16384], P('grp', 'row', 'col'), may hold values from -6 to 6
- factor_q: float32 [2, 16384, 256], P('grp', 'col', 'row'), may hold values from -0.046875 to 0.046875
- weights: float32 [2, 4096, 16384], P(None, 'row', ('col', 'grp')), may hold values from -6 to 6
- tokens: bfloat16 [256, 4096], P(None, 'row'), may hold values from -0.08984375 to 0.08984375
Outputs:
- momentum_out: float32 [2, 4096, 16384], P('grp', 'row', 'col')
- factor_out: float32 [2, 16384, 256], P('grp', 'col', 'row')
- weights_out: float32 [2, 4096, 16384], P(None, 'row', ('col', 'grp'))
- hidden: bfloat16 [256, 16384], P('row', ('col', 'grp'))
All inputs are finite; a program needn't handle non-finite values.
Results may differ from a plain program's by a relative error of at most 0.0061.
Values may be sent and summed in bfloat16 or wider, within the bound.
No kernel may reach another device: no remote copies, remote signals or barrier semaphores. Data moves between devices by JAX's collectives and lax.ppermute only.
A program may use at most 128 MiB of HBM per device.

v0:
```python
import math
import jax
import jax.numpy as jnp
from jax import lax
from jax.sharding import PartitionSpec as P

D = 4096
HID = 16384
feedback = 0.05
epsilon = 1e-06


def gram_of(left_rows):
    return jnp.dot(left_rows.T, left_rows, precision=lax.Precision.HIGHEST)


def orthonormal(gram_sum, left_rows):
    factor_l = jnp.linalg.cholesky(gram_sum)
    return jax.scipy.linalg.solve_triangular(factor_l, left_rows.T, lower=True).T


def local(momentum, gradient, factor_q, weights, tokens):
    buffer = momentum[0] + gradient[0].astype(jnp.float32)
    buffer_h = buffer.astype(jnp.bfloat16)
    partial_value = jnp.dot(
        buffer_h,
        lax.all_gather(factor_q[0].astype(jnp.bfloat16), "row", axis=1, tiled=True),
        preferred_element_type=jnp.float32,
    )
    left_full = lax.psum(partial_value, "col")
    gram_sum = lax.psum(gram_of(left_full), "row")
    left_h = orthonormal(gram_sum, left_full).astype(jnp.bfloat16)
    right_part = lax.dot_general(
        buffer_h, left_h, (((0,), (0,)), ((), ())), preferred_element_type=jnp.float32
    )
    rank_share = factor_q.shape[2]
    right_full = lax.psum(right_part, "row")
    squares = lax.psum(jnp.sum(right_full * right_full, axis=0), "col")
    new_q = right_full / jnp.sqrt(squares + epsilon)
    q_share = lax.dynamic_slice_in_dim(new_q, lax.axis_index("row") * rank_share, rank_share, 1)
    right_h = right_full.astype(jnp.bfloat16)
    new_q_h = new_q.astype(jnp.bfloat16)
    feedback_term = lax.dot_general(
        left_h, right_h, (((1,), (1,)), ((), ())), preferred_element_type=jnp.float32
    )
    mom_new = buffer - feedback * feedback_term
    left_both = lax.all_gather(left_h[None], "grp", axis=0, tiled=True)
    right_both = lax.all_to_all(new_q_h[None], "grp", split_axis=1, concat_axis=0, tiled=True)
    step_size = 0.4 * math.sqrt(max(D, HID))
    low_rank = lax.dot_general(
        left_both, right_both, (((2,), (2,)), ((0,), (0,))), preferred_element_type=jnp.float32
    )
    new_weights = weights - step_size * low_rank
    weights_h = new_weights.astype(jnp.bfloat16)
    dec_parts = lax.psum_scatter(
        jnp.einsum("bd,pdh->bph", tokens, weights_h, preferred_element_type=jnp.float32),
        "row",
        scatter_dimension=0,
        tiled=True,
    )
    hidden = (jax.nn.silu(dec_parts[:, 0]) * dec_parts[:, 1]).astype(jnp.bfloat16)
    return (mom_new[None], q_share[None], new_weights, hidden)


def solution(mesh):
    in_specs = (
        P("grp", "row", "col"),
        P("grp", "row", "col"),
        P("grp", "col", "row"),
        P(None, "row", ("col", "grp")),
        P(None, "row"),
    )
    out_specs = (
        P("grp", "row", "col"),
        P("grp", "col", "row"),
        P(None, "row", ("col", "grp")),
        P("row", ("col", "grp")),
    )
    return jax.shard_map(local, mesh=mesh, in_specs=in_specs, out_specs=out_specs, check_vma=False)
```

profile of v0, /device:TPU:0, one launch (start us, length us, event | category | flops | bytes accessed | tf_op | source)
XLA Modules:
  0.0 394.4 jit_solution(15597743867390131542)
XLA Ops:
  9.4 12.2 %all-gather.5.cloned.1.call-done = bf16[1,2048,256]{2,1,0:T(8,128)(2,1)} async-done(((bf16[1,2048,128]{2,1,0:T(8,128)(2,1)}), bf16[1,2048,256]{2,1,0:T(8,128)(2,1)}) %all-gather.5.cloned.1.call-update) | async-done | bytes 1048592 | tf_op jit(solution)/shard_map/all_gather | solution.py:27
  21.6 12.3 %fusion.9 = f32[2048,256]{1,0:T(8,128)} fusion(bf16[1,2048,256]{2,1,0:T(8,128)(2,1)} %all-gather.5.cloned.1.call-done, f32[1,2048,2048]{2,1,0:T(8,128)} %param.5, bf16[1,2048,2048]{2,1,0:T(8,128)(2,1)} %param.6), kind=kOutput, calls=%fused_computation.18 | convolution fusion | flops 2160066560 | bytes 28311552 | tf_op jit(solution)/shard_map/dot_general | solution.py:25
  34.0 103.6 %all-reduce.5.cloned.1.call-done = f32[2048,256]{1,0:T(8,128)} async-done(((f32[2048,256]{1,0:T(8,128)}), f32[2048,256]{1,0:T(8,128)}) %all-reduce.5.cloned.1.call-update) | async-done | bytes 2097168 | tf_op jit(solution)/shard_map/psum | solution.py:30
  137.6 6.4 %fusion.25 = f32[256,256]{0,1:T(8,128)} fusion(f32[2048,256]{1,0:T(8,128)} %all-reduce.5.cloned.1.call-done), kind=kOutput, calls=%fused_computation.56 | convolution fusion | flops 1610612736 | bytes 2359296 | tf_op jit(solution)/shard_map/dot_general | solution.py:14
  144.3 17.3 %all-reduce.7.cloned.1.call-done = f32[256,256]{0,1:T(8,128)} async-done(((f32[256,256]{0,1:T(8,128)}), f32[256,256]{0,1:T(8,128)}) %all-reduce.7.cloned.1.call-update) | async-done | bytes 262160 | tf_op jit(solution)/shard_map/psum | solution.py:31
  164.4 11.7 %cholesky.50 = f32[128,128]{1,0:T(8,128)S(1)} custom-call(f32[128,128]{1,0:T(8,128)S(1)} %cholesky.118), custom_call_target="Cholesky" | custom-call | tf_op jit(solution)/shard_map/jit(cholesky)/cholesky | solution.py:18
  176.2 9.8 %custom-call.15 = f32[1,128,128]{1,2,0:T(8,128)S(1)} custom-call(f32[1,128,128]{2,1,0:T(8,128)S(1)} %get-tuple-element.39), custom_call_target="InvertDiagBlocksLowerTriangular" | custom-call | tf_op jit(solution)/shard_map/jit(cholesky)/cholesky | solution.py:18
  188.2 11.7 %cholesky.105 = f32[128,128]{1,0:T(8,128)S(1)} custom-call(f32[128,128]{1,0:T(8,128)S(1)} %convolution_subtract_fusion.1), custom_call_target="Cholesky" | custom-call | tf_op jit(solution)/shard_map/jit(cholesky)/cholesky | solution.py:18
  203.0 5.7 %while.1 = (s32[]{:T(128)}, f32[256,256]{1,0:T(8,128)S(1)}, s32[2,2]{1,0:T(2,128)S(1)}, f32[2,128,128]{2,1,0:T(8,128)}, s32[]{:T(128)}) while((s32[]{:T(128)}, f32[256,256]{1,0:T(8,128)S(1)}, s32[2,2]{1,0:T(2,128)S(1)}, f32[2,128,128]{2,1,0:T(8,128)}, s32[]{:T(128)}) %tuple.32), condition=%wide.while_cond, body=%wide.while_body.sunk | while | flops 2 | bytes 132205 | solution.py:19
  208.8 20.5 %custom-call.16 = f32[2,128,128]{1,2,0:T(8,128)S(1)} custom-call(f32[2,128,128]{2,1,0:T(8,128)} %get-tuple-element.11), custom_call_target="InvertDiagBlocksLowerTriangular" | custom-call | tf_op jit(solution)/shard_map/jit(_solve_triangular)/triangular_solve | solution.py:19
  233.3 13.1 %fusion.15 = f32[2048,256]{1,0:T(8,128)} fusion(bf16[128,2048]{1,0:T(8,128)(2,1)S(1)} %convolution_convert_fusion, bf16[128,2048]{1,0:T(8,128)(2,1)S(1)} %get-tuple-element.42, f32[1,2048,2048]{2,1,0:T(8,128)} %param.5, bf16[1,2048,2048]{2,1,0:T(8,128)(2,1)} %param.6), kind=kOutput, calls=%fused_computation.29 | convolution fusion | flops 2162163712 | bytes 28311552 | tf_op jit(solution)/shard_map/dot_general | solution.py:33
  248.5 20.6 %all-reduce.9.cloned.1.call-done = f32[2048,256]{1,0:T(8,128)} async-done(((f32[2048,256]{1,0:T(8,128)}), f32[2048,256]{1,0:T(8,128)}) %all-reduce.9.cloned.1.call-update) | async-done | bytes 2097168 | tf_op jit(solution)/shard_map/psum | solution.py:37
  271.1 21.8 %psum.31 = f32[256]{0:T(256)S(1)} all-reduce(f32[256]{0:T(256)S(1)} %multiply_reduce_fusion), channel_id=1, replica_groups=mesh['row'=2,'col'=8,'grp'=2] {'col'}, use_global_device_ids=true, to_apply=%region_8.9 | all-reduce | flops 256 | bytes 2048 | tf_op jit(solution)/shard_map/psum | solution.py:38
  294.4 12.9 %copy.33 = bf16[1,2048,256]{2,0,1:T(2,128)(2,1)} copy(bf16[1,2048,256]{2,1,0:T(8,128)(2,1)S(1)} %get-tuple-element.32) | data formatting | bytes 2097152 | tf_op jit(solution)/shard_map/broadcast_in_dim | solution.py:48
  307.8 12.6 %reduce.12 = bf16[2048,256]{1,0:T(8,128)(2,1)} reduce(bf16[2048,1,256]{2,1,0:T(2,128)(2,1)} %bitcast.81, bf16[]{:T(256)} %broadcast.117), dimensions={1}, to_apply=%bitcast.70.reduce_sub_computation | reduce | bytes 2097154
  320.5 2.2 reshape.56
  322.6 4.4 %all-to-all-start = ((bf16[2,2,131072]{2,1,0:T(2,128)(2,1)}), bf16[2,2,131072]{2,1,0:T(2,128)(2,1)}, u32[]{:S(2)}, u32[]{:S(2)}) async-start(bf16[2,2,131072]{2,1,0:T(2,128)(2,1)} %reshape.56), calls=%async_computation | async-start | bytes 2097152 | tf_op jit(solution)/shard_map/all_to_all | solution.py:48
  327.1 4.3 %copy.30 = bf16[4096,256]{1,0:T(8,128)(2,1)} copy(bf16[4096,256]{0,1:T(8,128)(2,1)} %all-gather.7.cloned.1.call-done) | data formatting | bytes 4194304 | tf_op jit(solution)/shard_map/all_gather | solution.py:47
  331.4 6.3 %all-to-all-done = bf16[2,2,131072]{2,1,0:T(2,128)(2,1)} async-done(((bf16[2,2,131072]{2,1,0:T(2,128)(2,1)}), bf16[2,2,131072]{2,1,0:T(2,128)(2,1)}, u32[]{:S(2)}, u32[]{:S(2)}) %all-to-all-start) | async-done | bytes 1048608 | tf_op jit(solution)/shard_map/all_to_all | solution.py:48
  337.7 3.0 reshape.57
  342.9 14.3 %multiply_subtract_fusion = f32[2,2048,1024]{2,1,0:T(8,128)} fusion(f32[2,2048,1024]{2,1,0:T(8,128)} %param.8, bf16[2,2048,256]{2,1,0:T(8,128)(2,1)S(1)} %bitcast.79, bf16[2,1024,256]{2,1,0:T(8,128)(2,1)S(1)} %bitcast.82), kind=kOutput, calls=%fused_computation.5 | convolution fusion | flops 2155872256 | bytes 36700160 | tf_op jit(solution)/shard_map/dot_general | solution.py:50
  357.2 9.6 %fusion.3 = f32[256,2,1024]{0,2,1:T(8,128)} fusion(f32[2,2048,1024]{2,1,0:T(8,128)} %multiply_subtract_fusion, bf16[256,2048]{1,0:T(8,128)(2,1)S(1)} %copy-done), kind=kOutput, calls=%fused_computation.12 | convolution fusion | flops 2151677952 | bytes 19922944 | tf_op jit(solution)/shard_map/bd,pdh->bph/dot_general | solution.py:56
  366.9 2.4 dynamic-slice_bitcast_fusion
  369.2 15.9 %fusion = f32[1,2048,2048]{2,1,0:T(8,128)} fusion(f32[1,2048,2048]{2,1,0:T(8,128)} %param.5, bf16[1,2048,2048]{2,1,0:T(8,128)(2,1)} %param.6, f32[2048,256]{1,0:T(8,128)S(1)} %copy-done.1, bf16[128,2048]{1,0:T(8,128)(2,1)S(1)} %copy-done.4, bf16[128,2048]{1,0:T(8,128)(2,1)S(1)} %copy-done.7), kind=kOutput, calls=%fused_computation.4 | convolution fusion | flops 2166882304 | bytes 45088768 | tf_op jit(solution)/shard_map/dot_general | solution.py:43
  (67 shorter events, 29.3 us)
Async XLA Ops:
  7.2 350.1 %copy-start = (bf16[256,2048]{1,0:T(8,128)(2,1)S(1)}, bf16[256,2048]{1,0:T(8,128)(2,1)}, u32[]{:S(2)}) copy-start(bf16[256,2048]{1,0:T(8,128)(2,1)} %param.9) | copy-start | bytes 3145732
  7.2 14.5 %all-gather.5.cloned.1.call-start = ((), (), s32[]{:S(2)}) async-start(), calls=%async_computation.6 | async-start | bytes 1572864 | tf_op jit(solution)/shard_map/all_gather | solution.py:27
  9.4 128.2 %all-reduce.5.cloned.1.call-start = ((), (), s32[]{:S(2)}) async-start(), calls=%async_computation.2 | async-start | bytes 4194304 | tf_op jit(solution)/shard_map/psum | solution.py:30
  33.9 127.7 %all-reduce.7.cloned.1.call-start = ((), (), s32[]{:S(2)}) async-start(), calls=%async_computation.3 | async-start | bytes 524288 | tf_op jit(solution)/shard_map/psum | solution.py:31
  143.9 85.3 %copy-start.2 = (f32[2048,256]{1,0:T(8,128)S(1)}, f32[2048,256]{1,0:T(8,128)}, u32[]{:S(2)}) copy-start(f32[2048,256]{1,0:T(8,128)} %all-reduce.5.cloned.1.call-done) | copy-start | bytes 6291460
  144.0 125.1 %all-reduce.9.cloned.1.call-start = ((), (), s32[]{:S(2)}) async-start(), calls=%async_computation.4 | async-start | bytes 4194304 | tf_op jit(solution)/shard_map/psum | solution.py:37
  163.7 0.7 copy-start.10
  199.9 2.0 copy-start.9
  230.3 2.9 copy-start.5
  233.3 13.2 %copy-start.3 = (bf16[128,2048]{1,0:T(8,128)(2,1)}, bf16[128,2048]{1,0:T(8,128)(2,1)S(1)}, u32[]{:S(2)}) copy-start(bf16[128,2048]{1,0:T(8,128)(2,1)S(1)} %convolution_convert_fusion) | copy-start | bytes 1572868
  246.4 1.0 copy-start.6
  246.4 80.7 %all-gather.7.cloned.1.call-start = ((), (), s32[]{:S(2)}) async-start(), calls=%async_computation.7 | async-start | bytes 3145728 | tf_op jit(solution)/shard_map/all_gather | solution.py:47
  269.1 23.8 %copy-start.1 = (f32[2048,256]{1,0:T(8,128)S(1)}, f32[2048,256]{1,0:T(8,128)}, u32[]{:S(2)}) copy-start(f32[2048,256]{1,0:T(8,128)} %all-reduce.9.cloned.1.call-done) | copy-start | bytes 6291460
  322.6 15.1 %all-to-all-start = ((bf16[2,2,131072]{2,1,0:T(2,128)(2,1)}), bf16[2,2,131072]{2,1,0:T(2,128)(2,1)}, u32[]{:S(2)}, u32[]{:S(2)}) async-start(bf16[2,2,131072]{2,1,0:T(2,128)(2,1)} %reshape.56), calls=%async_computation | async-start | bytes 2097152 | tf_op jit(solution)/shard_map/all_to_all | solution.py:48
  327.1 58.0 %reduce-scatter.2.cloned.1.call-start = ((), (), s32[]{:S(2)}) async-start(), calls=%async_computation.5 | async-start | bytes 3145728 | tf_op jit(solution)/shard_map/reduce_scatter | solution.py:55
  340.7 2.2 copy-start.8
  366.8 2.4 copy-start.4
  366.9 2.4 copy-start.7
Sparse Core Ops, SparseCore 0:
  10.1 11.4 all-gather.4
  34.0 103.4 all-reduce.4
  144.1 17.4 all-reduce.6
  246.5 22.4 all-reduce.8
  271.0 34.2 all-gather.6
  367.0 5.6 reduce-scatter.1
where the time goes:
time: 400 us; the launch traced here: 394 us
  waiting for transfers between devices  160 us (40%)
  matrix products  77.6 us (19%)
  other arithmetic  77.2 us (19%)
  local copies, waits for them, and re-layouts  36.3 us (9%)
  blocking collectives  21.8 us (5%)
  between operations  15.9 us (4%)
  starting transfers between devices  4.96 us (1%)
    psum x1, waiting for transfers between devices, local(): left_full = lax.psum(partial_value, 'col')  104 us
    another operation x6, other arithmetic, orthonormal(): factor_l = jnp.linalg.cholesky(gram_sum)  34 us
    psum x1, blocking collectives, local(): squares = lax.psum(jnp.sum(right_full * right_full, axis=0), 'col')  21.8 us
    another operation x3, other arithmetic, orthonormal(): jax.scipy.linalg.solve_triangular(factor_l, left_rows.T, lower=True)  21.5 us
    psum x1, waiting for transfers between devices, local(): right_full = lax.psum(right_part, 'row')  20.6 us
    psum x1, waiting for transfers between devices, local(): gram_sum = lax.psum(gram_of(left_full), 'row')  17.3 us
    dot_general x1, matrix products, local(): lax.dot_general(left_h, right_h, (((1,), (1,)), ((), ())), preferred_elem...  15.9 us
    dot_general x1, matrix products, local(): lax.dot_general(left_both, right_both, (((2,), (2,)), ((0,), (0,))), pref...  14.3 us
  transfers between devices with their start and end apart: 7, of which 5 were waited for; matrix products, arithmetic and copies ran while one was open for 14% of the time, Pallas kernels for 0%

commit v1 on v0

--- a/solution.py
+++ b/solution.py
@@ -27,7 +27,7 @@
         lax.all_gather(factor_q[0].astype(jnp.bfloat16), "row", axis=1, tiled=True),
         preferred_element_type=jnp.float32,
     )
-    left_full = lax.psum(partial_value, "col")
+    left_full = jnp.sum(lax.all_gather(partial_value, "col"), axis=0)
     gram_sum = lax.psum(gram_of(left_full), "row")
     left_h = orthonormal(gram_sum, left_full).astype(jnp.bfloat16)
     right_part = lax.dot_general(

time: 400 us -> 526 us (1.31)
  waiting for transfers between devices: 160 us -> 283 us
  other arithmetic: 77.2 us -> 83 us
    all_gather x0 -> x1, waiting for transfers between devices: none -> 229 us  [local(): left_full = jnp.sum(lax.all_gather(partial_value, 'col'), axis=0)]
    psum x1 -> x0, waiting for transfers between devices: 104 us -> none  [local(): left_full = lax.psum(partial_value, 'col')]
    reduce_sum x0 -> x1, other arithmetic: none -> 7.14 us  [local(): left_full = jnp.sum(lax.all_gather(partial_value, 'col'), axis=0)]
  transfers between devices with their start and end apart: 7 -> 7, of which waited for: 5 -> 5; matrix products, arithmetic and copies ran while one was open for 14% -> 11% of each run, Pallas kernels for 0% -> 0%
where the time goes in v1:
time: 526 us; the launch traced here: 519 us
  waiting for transfers between devices  283 us (54%)
  other arithmetic  83 us (16%)
  matrix products  75.5 us (14%)
  local copies, waits for them, and re-layouts  35.2 us (7%)
  blocking collectives  21.8 us (4%)
  between operations  15.8 us (3%)
    all_gather x1, waiting for transfers between devices, local(): left_full = jnp.sum(lax.all_gather(partial_value, 'col'), axis=0)  229 us
    another operation x6, other arithmetic, orthonormal(): factor_l = jnp.linalg.cholesky(gram_sum)  33.9 us
    psum x1, blocking collectives, local(): squares = lax.psum(jnp.sum(right_full * right_full, axis=0), 'col')  21.8 us
    psum x1, waiting for transfers between devices, local(): right_full = lax.psum(right_part, 'row')  21.5 us
    another operation x3, other arithmetic, orthonormal(): jax.scipy.linalg.solve_triangular(factor_l, left_rows.T, lower=True)  20.2 us
    dot_general x1, matrix products, local(): lax.dot_general(left_h, right_h, (((1,), (1,)), ((), ())), preferred_elem...  15.9 us
    psum x1, waiting for transfers between devices, local(): gram_sum = lax.psum(gram_of(left_full), 'row')  14.4 us
    dot_general x1, matrix products, local(): lax.dot_general(left_both, right_both, (((2,), (2,)), ((0,), (0,))), pref...  14.3 us
  transfers between devices with their start and end apart: 7, of which 5 were waited for; matrix products, arithmetic and copies ran while one was open for 11% of the time, Pallas kernels for 0%

profile of v1, /device:TPU:0, one launch (start us, length us, event | category | flops | bytes accessed | tf_op | source)
XLA Modules:
  0.0 519.4 jit_solution(2016915493409201162)
XLA Ops:
  9.4 12.2 %all-gather.7.cloned.1.call-done = bf16[1,2048,256]{2,1,0:T(8,128)(2,1)} async-done(((bf16[1,2048,128]{2,1,0:T(8,128)(2,1)}), bf16[1,2048,256]{2,1,0:T(8,128)(2,1)}) %all-gather.7.cloned.1.call-update) | async-done | bytes 1048592 | tf_op jit(solution)/shard_map/all_gather | solution.py:27
  21.6 12.3 %fusion.9 = f32[2048,256]{1,0:T(8,128)} fusion(bf16[1,2048,256]{2,1,0:T(8,128)(2,1)} %all-gather.7.cloned.1.call-done, f32[1,2048,2048]{2,1,0:T(8,128)} %param.5, bf16[1,2048,2048]{2,1,0:T(8,128)(2,1)} %param.6), kind=kOutput, calls=%fused_computation.18 | convolution fusion | flops 2160066560 | bytes 28311552 | tf_op jit(solution)/shard_map/dot_general | solution.py:25
  34.0 228.6 %all-gather.9.cloned.1.call-done = f32[16384,256]{1,0:T(8,128)} async-done(((f32[2048,256]{1,0:T(8,128)}), f32[16384,256]{1,0:T(8,128)}) %all-gather.9.cloned.1.call-update) | async-done | bytes 16777232 | tf_op jit(solution)/shard_map/all_gather | solution.py:30
  262.6 7.1 %reduce_sum.18 = f32[2048,256]{1,0:T(8,128)S(1)} reduce(f32[8,2048,256]{2,1,0:T(8,128)} %bitcast.78, f32[]{:T(128)} %constant.87.clone.1), dimensions={0}, to_apply=%region_0.0 | reduce | flops 3670016 | bytes 18874372 | tf_op jit(solution)/shard_map/reduce_sum | solution.py:30
  269.7 4.2 fusion.25
  276.1 14.4 %all-reduce.4.cloned.1.call-done = f32[256,256]{0,1:T(8,128)} async-done(((f32[256,256]{0,1:T(8,128)}), f32[256,256]{0,1:T(8,128)}) %all-reduce.4.cloned.1.call-update) | async-done | bytes 262160 | tf_op jit(solution)/shard_map/psum | solution.py:31
  292.5 11.7 %cholesky.50 = f32[128,128]{1,0:T(8,128)S(1)} custom-call(f32[128,128]{1,0:T(8,128)S(1)} %cholesky.118), custom_call_target="Cholesky" | custom-call | tf_op jit(solution)/shard_map/jit(cholesky)/cholesky | solution.py:18
  304.3 9.8 %custom-call.15 = f32[1,128,128]{1,2,0:T(8,128)S(1)} custom-call(f32[1,128,128]{2,1,0:T(8,128)S(1)} %get-tuple-element.43), custom_call_target="InvertDiagBlocksLowerTriangular" | custom-call | tf_op jit(solution)/shard_map/jit(cholesky)/cholesky | solution.py:18
  314.6 11.7 %cholesky.105 = f32[128,128]{1,0:T(8,128)S(1)} custom-call(f32[128,128]{1,0:T(8,128)S(1)} %convolution_subtract_fusion.1), custom_call_target="Cholesky" | custom-call | tf_op jit(solution)/shard_map/jit(cholesky)/cholesky | solution.py:18
  328.4 4.0 while.1
  332.4 20.2 %custom-call.16 = f32[2,128,128]{1,2,0:T(8,128)S(1)} custom-call(f32[2,128,128]{2,1,0:T(8,128)S(1)} %get-tuple-element.11), custom_call_target="InvertDiagBlocksLowerTriangular" | custom-call | tf_op jit(solution)/shard_map/jit(_solve_triangular)/triangular_solve | solution.py:19
  354.9 2.4 convolution_subtract_fusion
  358.4 13.1 %fusion.15 = f32[2048,256]{1,0:T(8,128)} fusion(bf16[128,2048]{1,0:T(8,128)(2,1)S(1)} %convolution_convert_fusion, bf16[128,2048]{1,0:T(8,128)(2,1)S(1)} %get-tuple-element.46, f32[1,2048,2048]{2,1,0:T(8,128)} %param.5, bf16[1,2048,2048]{2,1,0:T(8,128)(2,1)} %param.6), kind=kOutput, calls=%fused_computation.29 | convolution fusion | flops 2162163712 | bytes 28311552 | tf_op jit(solution)/shard_map/dot_general | solution.py:33
  372.6 21.5 %all-reduce.6.cloned.1.call-done = f32[2048,256]{1,0:T(8,128)} async-done(((f32[2048,256]{1,0:T(8,128)}), f32[2048,256]{1,0:T(8,128)}) %all-reduce.6.cloned.1.call-update) | async-done | bytes 2097168 | tf_op jit(solution)/shard_map/psum | solution.py:37
  396.2 21.8 %psum.23 = f32[256]{0:T(256)S(1)} all-reduce(f32[256]{0:T(256)S(1)} %multiply_reduce_fusion), channel_id=1, replica_groups=mesh['row'=2,'col'=8,'grp'=2] {'col'}, use_global_device_ids=true, to_apply=%region_8.9 | all-reduce | flops 256 | bytes 2048 | tf_op jit(solution)/shard_map/psum | solution.py:38
  419.5 12.9 %copy.38 = bf16[1,2048,256]{2,0,1:T(2,128)(2,1)} copy(bf16[1,2048,256]{2,1,0:T(8,128)(2,1)S(1)} %get-tuple-element.36) | data formatting | bytes 2097152 | tf_op jit(solution)/shard_map/broadcast_in_dim | solution.py:48
  432.9 12.6 %reduce.12 = bf16[2048,256]{1,0:T(8,128)(2,1)} reduce(bf16[2048,1,256]{2,1,0:T(2,128)(2,1)} %bitcast.83, bf16[]{:T(256)} %broadcast.117), dimensions={1}, to_apply=%bitcast.71.reduce_sub_computation | reduce | bytes 2097154
  447.7 4.4 all-to-all-start
  452.2 4.3 copy.35
  456.5 6.3 %all-to-all-done = bf16[2,2,131072]{2,1,0:T(2,128)(2,1)} async-done(((bf16[2,2,131072]{2,1,0:T(2,128)(2,1)}), bf16[2,2,131072]{2,1,0:T(2,128)(2,1)}, u32[]{:S(2)}, u32[]{:S(2)}) %all-to-all-start) | async-done | bytes 1048608 | tf_op jit(solution)/shard_map/all_to_all | solution.py:48
  462.8 3.0 reshape.58
  467.9 14.3 %multiply_subtract_fusion = f32[2,2048,1024]{2,1,0:T(8,128)} fusion(f32[2,2048,1024]{2,1,0:T(8,128)} %param.8, bf16[2,2048,256]{2,1,0:T(8,128)(2,1)S(1)} %bitcast.79, bf16[2,1024,256]{2,1,0:T(8,128)(2,1)S(1)} %bitcast.84), kind=kOutput, calls=%fused_computation.5 | convolution fusion | flops 2155872256 | bytes 36700160 | tf_op jit(solution)/shard_map/dot_general | solution.py:50
  482.3 9.6 %fusion.3 = f32[256,2,1024]{0,2,1:T(8,128)} fusion(f32[2,2048,1024]{2,1,0:T(8,128)} %multiply_subtract_fusion, bf16[256,2048]{1,0:T(8,128)(2,1)S(1)} %copy-done), kind=kOutput, calls=%fused_computation.12 | convolution fusion | flops 2151677952 | bytes 19922944 | tf_op jit(solution)/shard_map/bd,pdh->bph/dot_general | solution.py:56
  494.2 15.9 %fusion = f32[1,2048,2048]{2,1,0:T(8,128)} fusion(f32[1,2048,2048]{2,1,0:T(8,128)} %param.5, bf16[1,2048,2048]{2,1,0:T(8,128)(2,1)} %param.6, f32[2048,256]{1,0:T(8,128)S(1)} %copy-done.1, bf16[128,2048]{1,0:T(8,128)(2,1)S(1)} %copy-done.3, bf16[128,2048]{1,0:T(8,128)(2,1)S(1)} %copy-done.5), kind=kOutput, calls=%fused_computation.4 | convolution fusion | flops 2166882304 | bytes 45088768 | tf_op jit(solution)/shard_map/dot_general | solution.py:43
  (61 shorter events, 29.3 us)
Async XLA Ops:
  7.2 475.1 %copy-start = (bf16[256,2048]{1,0:T(8,128)(2,1)S(1)}, bf16[256,2048]{1,0:T(8,128)(2,1)}, u32[]{:S(2)}) copy-start(bf16[256,2048]{1,0:T(8,128)(2,1)} %param.9) | copy-start | bytes 3145732
  7.2 14.5 %all-gather.7.cloned.1.call-start = ((), (), s32[]{:S(2)}) async-start(), calls=%async_computation.5 | async-start | bytes 1572864 | tf_op jit(solution)/shard_map/all_gather | solution.py:27
  9.4 253.2 %all-gather.9.cloned.1.call-start = ((), (), s32[]{:S(2)}) async-start(), calls=%async_computation.6 | async-start | bytes 18874368 | tf_op jit(solution)/shard_map/all_gather | solution.py:30
  33.9 256.5 %all-reduce.4.cloned.1.call-start = ((), (), s32[]{:S(2)}) async-start(), calls=%async_computation.2 | async-start | bytes 524288 | tf_op jit(solution)/shard_map/psum | solution.py:31
  273.9 120.3 %all-reduce.6.cloned.1.call-start = ((), (), s32[]{:S(2)}) async-start(), calls=%async_computation.3 | async-start | bytes 4194304 | tf_op jit(solution)/shard_map/psum | solution.py:37
  354.9 16.7 %copy-start.4 = (bf16[128,2048]{1,0:T(8,128)(2,1)}, bf16[128,2048]{1,0:T(8,128)(2,1)S(1)}, u32[]{:S(2)}) copy-start(bf16[128,2048]{1,0:T(8,128)(2,1)S(1)} %get-tuple-element.46) | copy-start | bytes 1572868
  358.4 13.2 %copy-start.2 = (bf16[128,2048]{1,0:T(8,128)(2,1)}, bf16[128,2048]{1,0:T(8,128)(2,1)S(1)}, u32[]{:S(2)}) copy-start(bf16[128,2048]{1,0:T(8,128)(2,1)S(1)} %convolution_convert_fusion) | copy-start | bytes 1572868
  371.5 80.7 %all-gather.11.cloned.1.call-start = ((), (), s32[]{:S(2)}) async-start(), calls=%async_computation.7 | async-start | bytes 3145728 | tf_op jit(solution)/shard_map/all_gather | solution.py:47
  394.2 23.8 %copy-start.1 = (f32[2048,256]{1,0:T(8,128)S(1)}, f32[2048,256]{1,0:T(8,128)}, u32[]{:S(2)}) copy-start(f32[2048,256]{1,0:T(8,128)} %all-reduce.6.cloned.1.call-done) | copy-start | bytes 6291460
  447.7 15.1 %all-to-all-start = ((bf16[2,2,131072]{2,1,0:T(2,128)(2,1)}), bf16[2,2,131072]{2,1,0:T(2,128)(2,1)}, u32[]{:S(2)}, u32[]{:S(2)}) async-start(bf16[2,2,131072]{2,1,0:T(2,128)(2,1)} %reshape.57), calls=%async_computation | async-start | bytes 2097152 | tf_op jit(solution)/shard_map/all_to_all | solution.py:48
  452.1 58.0 %reduce-scatter.2.cloned.1.call-start = ((), (), s32[]{:S(2)}) async-start(), calls=%async_computation.4 | async-start | bytes 3145728 | tf_op jit(solution)/shard_map/reduce_scatter | solution.py:55
  465.7 2.2 copy-start.6
  491.9 2.4 copy-start.3
  491.9 2.4 copy-start.5
Sparse Core Ops, SparseCore 0:
  10.1 11.4 all-gather.6
  34.0 228.4 all-gather.8
  274.0 16.3 all-reduce.3
  371.6 22.4 all-reduce.5
  396.1 34.2 all-gather.10
  492.0 5.6 reduce-scatter.1
